TPU v7x, 32 devices: a whole 2x2x4 slice. The times are simulated.
32 devices in a mesh: row: 8 (over y, x, core), col: 4 (over z).
Axes of the slice: x: 2, y: 2, z: 4, core: 2. Of those that a mesh axis runs over, the one named last changes fastest.
Arguments:
- design: bfloat16 [4096, 6144], P(('row', 'col')), may hold values from -0.09375 to 0.09375
- observations: float32 [4096], P(('row', 'col')), may hold values from -6 to 6
- gaps: int32 [4096], P(('row', 'col')), may hold values 0 or 1
- noise_var: float32 [4096], P(('row', 'col')), may hold values from 0.25 to 4
- arc_lengths: int32 [32, 4], P(('row', 'col')), may hold values from 1 to 64, 128 in all within a row
- arc_amp: float32 [32, 4], P(('row', 'col')), may hold values from 0.2 to 2
- arc_decay: float32 [32, 4], P(('row', 'col')), may hold values from 0.3 to 0.95
- plan: int32 [32], P(('row', 'col')), may hold values from 0 to 31, each once
- tile_map: int32 [48], replicated, may hold values from 0 to 47, each once
Outputs:
- gram: float32 [6144, 6144], P('row', 'col')
- normal_rhs: float32 [6144], P('row')
- balanced_obs: float32 [32, 128], P(('row', 'col'))
Inputs may be any that keep to these rules, and one draw needn't show every extreme that they name: `plan`: a permutation of the blocks. `tile_map`: a permutation of the tiles. `arc_lengths`: each block's arc lengths sum to 128; some arc has 64 rows.
All inputs are finite; a program needn't handle non-finite values. No bound on the sum of `gaps` on one device may be relied on, other than what follows from the above.
Results may differ from a plain program's by a relative error of at most 0.004.
Values may be sent and summed in bfloat16 or wider, within the bound.
A program may use at most 192 MiB of HBM per device.

v0:
```python
import jax
import jax.numpy as jnp
from jax import lax
from jax.sharding import PartitionSpec as P


def whiten(block, obs_rows, live_rows, noise_rows, lengths, amplitude, decay):
    block_rows = block.shape[0]
    arc_count = lengths.shape[0]
    position = jnp.arange(block_rows, dtype=jnp.int32)
    arc_ends = jnp.cumsum(lengths)
    arc_id = jnp.sum((arc_ends[None, :] <= position[:, None]).astype(jnp.int32), axis=1)
    member = (arc_id[:, None] == jnp.arange(arc_count, dtype=jnp.int32)[None, :]).astype(
        jnp.float32
    )
    row_amp = jnp.sum(member * amplitude[None, :], axis=1)
    row_rate = jnp.sum(member * jnp.log(decay)[None, :], axis=1)
    same_arc = (arc_id[:, None] == arc_id[None, :]).astype(jnp.float32)
    row_lag = jnp.abs(position[:, None] - position[None, :]).astype(jnp.float32)
    kernel = (
        row_amp[:, None]
        * jnp.exp(row_lag * row_rate[:, None])
        * same_arc
        * live_rows[:, None]
        * live_rows[None, :]
    )
    covariance = kernel + jnp.diag(noise_rows)
    factor = jnp.linalg.cholesky(covariance)
    solved = lax.linalg.triangular_solve(
        factor, block.astype(jnp.float32) * live_rows[:, None], left_side=True, lower=True
    )
    solved_obs = lax.linalg.triangular_solve(
        factor, (obs_rows * live_rows)[:, None], left_side=True, lower=True
    )
    return (solved.astype(jnp.bfloat16), solved_obs[:, 0])


def on_device(
    design, observations, gaps, noise_var, arc_lengths, arc_amp, arc_decay, plan, tile_map
):
    block_count = arc_lengths.shape[0]
    block_rows = design.shape[0] // block_count
    columns = design.shape[1]
    tile_count = tile_map.shape[0]
    tile_size = columns // tile_count
    local_rows = block_count * block_rows
    live_rows = gaps.astype(jnp.float32)
    white, white_obs = jax.vmap(whiten)(
        design.reshape(block_count, block_rows, columns),
        observations.reshape(block_count, block_rows),
        live_rows.reshape(block_count, block_rows),
        noise_var.reshape(block_count, block_rows),
        arc_lengths,
        arc_amp,
        arc_decay,
    )
    slotted = jnp.take(white.reshape(local_rows, tile_count, tile_size), tile_map, axis=1)
    obs_every = lax.all_gather(white_obs.reshape(local_rows), ("row", "col"), axis=0, tiled=True)
    total_rows = obs_every.shape[0]
    row_devices = lax.axis_size("row")
    col_devices = lax.axis_size("col")
    row_tiles = tile_count // row_devices
    col_tiles = tile_count // col_devices
    own_rows = lax.all_to_all(slotted, "row", split_axis=1, concat_axis=0, tiled=True)
    row_panel = lax.all_gather(own_rows, "col", axis=0, tiled=True)
    row_panel = row_panel.reshape(col_devices, row_devices, local_rows, row_tiles * tile_size)
    row_panel = jnp.swapaxes(row_panel, 0, 1).reshape(total_rows, row_tiles * tile_size)
    own_cols = lax.all_to_all(slotted, "col", split_axis=1, concat_axis=0, tiled=True)
    shard_piece = lax.all_gather(own_cols, "row", axis=0, tiled=True)
    piece_rows = shard_piece.shape[0]
    flat_piece = shard_piece.reshape(piece_rows, col_tiles * tile_size)
    gram = lax.dot_general(
        row_panel, flat_piece, (((0,), (0,)), ((), ())), preferred_element_type=jnp.float32
    )
    obs_half = obs_every.astype(jnp.bfloat16)
    normal_rhs = jnp.dot(obs_half, row_panel, preferred_element_type=jnp.float32)
    balanced_obs = jnp.take(obs_every.reshape(-1, block_rows), plan, axis=0)
    return (gram, normal_rhs, balanced_obs)


def solution(mesh):
    placed = (
        P(("row", "col"), None),
        P(("row", "col")),
        P(("row", "col")),
        P(("row", "col")),
        P(("row", "col"), None),
        P(("row", "col"), None),
        P(("row", "col"), None),
        P(("row", "col")),
        P(),
    )
    return jax.shard_map(
        on_device,
        mesh=mesh,
        in_specs=placed,
        out_specs=(P("row", "col"), P("row"), P(("row", "col"), None)),
        check_vma=False,
    )
```

profile of v0, /device:TPU:8, one launch (start us, length us, event | category | flops | bytes accessed | tf_op | source)
XLA Modules:
  0.0 322.3 jit_solution(9754379693509585326)
XLA Ops:
  7.2 0.7 compare_and_fusion
  7.9 0.7 compare_select_fusion
  8.5 0.7 convert_element_type.39
  9.2 0.8 reduce_window_sum.11
  10.0 0.1 convert_reduce_fusion
  10.1 0.7 log_bitcast_fusion
  10.8 0.7 select_reduce_fusion.2
  11.5 0.8 select_add_fusion
  12.3 0.1 copy.28
  12.4 0.8 fusion.9
  13.2 11.7 %custom-call.9 = f32[1,128,128]{2,1,0:T(8,128)S(1)} custom-call(f32[1,128,128]{2,1,0:T(8,128)S(1)} %fusion.9), custom_call_target="Cholesky" | custom-call | tf_op jit(solution)/shard_map/vmap(jit(cholesky))/cholesky | solution.py:28
  25.0 0.6 compare_reduce_fusion
  25.6 0.7 fusion.6
  26.3 9.8 %custom-call.10 = f32[1,1,128,128]{2,3,1,0:T(8,128)S(1)} custom-call(f32[1,1,128,128]{3,2,1,0:T(8,128)S(1)} %fusion.6), custom_call_target="InvertDiagBlocksLowerTriangular" | custom-call | tf_op jit(solution)/shard_map/vmap()/triangular_solve | solution.py:29
  36.1 4.3 %fusion.3 = bf16[16,48,8,128]{3,2,1,0:T(8,128)(2,1)S(1)} fusion(bf16[128,6144]{1,0:T(8,128)(2,1)} %param.9, f32[128]{0:T(128)S(1)} %convert_element_type.39, f32[1,1,128,128]{2,3,1,0:T(8,128)S(1)} %custom-call.10), kind=kOutput, calls=%fused_computation.7 | convolution fusion | flops 1210318848 | bytes 3211776 | tf_op jit(solution)/shard_map/vmap()/triangular_solve | solution.py:29
  40.4 0.4 copy.39
  40.9 0.9 gather_fusion
  41.8 0.2 select_bitcast_fusion
  42.0 24.5 %all_to_all.36 = bf16[128,48,128]{2,0,1:T(8,128)(2,1)S(1)} all-to-all(bf16[128,48,128]{2,0,1:T(8,128)(2,1)S(1)} %select_bitcast_fusion), channel_id=1, replica_groups=mesh['row'=8,'col'=4] {'row'}, dimensions={1} | all-to-all | bytes 3145728 | tf_op jit(solution)/shard_map/all_to_all | solution.py:64
  66.4 1.2 copy.30
  67.8 80.1 %all_to_all.37 = bf16[128,48,128]{2,0,1:T(8,128)(2,1)S(1)} all-to-all(bf16[128,48,128]{2,0,1:T(8,128)(2,1)S(1)} %select_bitcast_fusion), channel_id=1, replica_groups=mesh['row'=8,'col'=4] {'col'}, dimensions={1} | all-to-all | bytes 3145728 | tf_op jit(solution)/shard_map/all_to_all | solution.py:68
  147.9 1.3 copy.33
  149.8 0.2 convolution_bitcast_fusion
  150.0 70.0 %all-gather = f32[32,1,128]{2,1,0:T(1,128)S(1)} all-gather(f32[1,1,128]{2,1,0:T(1,128)S(1)} %convolution_bitcast_fusion), channel_id=1, replica_groups=mesh['row'=8,'col'=4] {'row','col'}, dimensions={0}, use_global_device_ids=true | all-gather | bytes 16896 | tf_op jit(solution)/shard_map/all_gather | solution.py:58
  220.0 0.5 fusion.10
  220.5 9.0 %copy.31 = bf16[4096,6,128]{0,2,1:T(8,128)(2,1)} copy(bf16[4096,6,128]{2,0,1:T(8,128)(2,1)} %all-gather.4.cloned.1.call-done) | data formatting | bytes 12582912 | tf_op jit(solution)/shard_map/all_gather | solution.py:65
  229.5 7.4 %copy.37 = bf16[96,8,32,128]{3,2,1,0:T(8,128)(2,1)} copy(bf16[96,8,32,128]{3,1,2,0:T(8,128)(2,1)} %bitcast.60) | data formatting | bytes 12582912
  236.9 9.1 %copy.32 = bf16[8,4,128,768]{3,2,1,0:T(8,128)(2,1)} copy(bf16[8,4,128,768]{2,0,1,3:T(8,128)(2,1)} %bitcast.61) | data formatting | bytes 12582912 | tf_op jit(solution)/shard_map/transpose | solution.py:67
  246.0 4.9 %convolution_reduce_fusion = f32[768]{0:T(1024)} fusion(bf16[4096,1]{0,1:T(2,128)(2,1)S(1)} %reshape.535, bf16[4096,768]{1,0:T(8,128)(2,1)} %bitcast.58), kind=kOutput, calls=%fused_computation.8 | convolution fusion | flops 6291456 | bytes 6302720 | tf_op jit(solution)/shard_map/dot_general | solution.py:76
  250.9 31.5 %all-gather.6.cloned.1.call-done = bf16[4096,12,128]{2,0,1:T(8,128)(2,1)} async-done(((bf16[512,12,128]{2,0,1:T(8,128)(2,1)}), bf16[4096,12,128]{2,0,1:T(8,128)(2,1)}) %all-gather.6.cloned.1.call-update) | async-done | bytes 12582928 | tf_op jit(solution)/shard_map/all_gather | solution.py:69
  282.5 16.8 %copy.34 = bf16[4096,12,128]{0,2,1:T(8,128)(2,1)} copy(bf16[4096,12,128]{2,0,1:T(8,128)(2,1)} %all-gather.6.cloned.1.call-done) | data formatting | bytes 25165824 | tf_op jit(solution)/shard_map/all_gather | solution.py:69
  299.3 16.2 %fusion.14 = f32[768,1536]{1,0:T(8,128)} fusion(bf16[4096,768]{1,0:T(8,128)(2,1)} %bitcast.59, bf16[4096,1536]{0,1:T(8,128)(2,1)} %bitcast.62), kind=kOutput, calls=%fused_computation.36 | convolution fusion | flops 9663676416 | bytes 23592960 | tf_op jit(solution)/shard_map/dot_general | solution.py:72
  (13 shorter events, 0.2 us)
Async XLA Ops:
  7.2 213.3 %all-gather.4.cloned.1.call-start = ((), (), s32[]{:S(2)}) async-start(), calls=%async_computation.2 | async-start | bytes 7864320 | tf_op jit(solution)/shard_map/all_gather | solution.py:65
  67.7 214.8 %all-gather.6.cloned.1.call-start = ((), (), s32[]{:S(2)}) async-start(), calls=%async_computation.3 | async-start | bytes 14155776 | tf_op jit(solution)/shard_map/all_gather | solution.py:69
  147.9 2.0 copy-start
  147.9 2.0 copy-start.1
Sparse Core Ops, SparseCore 0:
  67.8 139.8 all-gather.3
  209.6 72.8 all-gather.5
where the time goes:
time: 325 us; the launch traced here: 322 us
  blocking collectives  175 us (54%)
  local copies, waits for them, and re-layouts  46.9 us (14%)
  waiting for transfers between devices  31.6 us (10%)
  other arithmetic  28.8 us (9%)
  matrix products  25.6 us (8%)
  between operations  14.8 us (5%)
    all_to_all x1, blocking collectives, on_device(): lax.all_to_all(slotted, 'col', split_axis=1, concat_axis=0, tiled=True)  80.1 us
    all_gather x1, blocking collectives, on_device(): lax.all_gather(white_obs.reshape(local_rows), ('row', 'col'), axis=0, til...  70 us
    all_gather x1, waiting for transfers between devices, on_device(): shard_piece = lax.all_gather(own_cols, 'row', axis=0, tiled=True)  31.5 us
    all_to_all x1, blocking collectives, on_device(): lax.all_to_all(slotted, 'row', split_axis=1, concat_axis=0, tiled=True)  24.5 us
    all_gather x1, local copies, waits for them, and re-layouts, on_device(): shard_piece = lax.all_gather(own_cols, 'row', axis=0, tiled=True)  16.8 us
    dot_general x1, matrix products, on_device(): lax.dot_general(row_panel, flat_piece, (((0,), (0,)), ((), ())), preferre...  16.2 us
    another operation x3, other arithmetic, whiten(): factor = jnp.linalg.cholesky(covariance)  12.4 us
    another operation x2, other arithmetic, whiten(): lax.linalg.triangular_solve(factor, block.astype(jnp.float32) * live_rows...  10.5 us
  transfers between devices with their start and end apart: 2, of which 1 were waited for; matrix products, arithmetic and copies ran while one was open for 10% of the time, Pallas kernels for 0%

commit v1 on v0

v1 whole, which is shorter than its diff:
```python
import functools

import jax
import jax.numpy as jnp
from jax import lax
from jax.experimental import pallas as pl
from jax.experimental.pallas import tpu as pltpu
from jax.sharding import PartitionSpec as P

MESH = pl.DeviceIdType.MESH
EXTRA = 16


def by_row(vector, rows):
    return jnp.transpose(jnp.broadcast_to(vector, (rows, vector.shape[1])))


def whiten_kernel(
    arcs, tile_map, lengths, amps, decays, design, obs, gaps, noise,
    white, white_t, live_m, noise_m, phi_m, amp_m, start_m, inno_m, var_m, parts,
):
    rows = design.shape[0]
    slots_z = white.shape[0] * white.shape[1] * white.shape[3] // rows
    half_tiles = white.shape[3] // rows
    row_tiles = (white_t.shape[1] - EXTRA) // rows
    live_row = gaps[...].astype(jnp.float32)
    live_m[...] = by_row(live_row, rows)
    noise_m[...] = by_row(noise[...], rows)
    position = lax.broadcasted_iota(jnp.int32, (rows, rows), 0)
    lane = lax.broadcasted_iota(jnp.int32, (rows, rows), 1)
    phi = jnp.zeros((rows, rows), jnp.float32)
    amp = jnp.zeros((rows, rows), jnp.float32)
    first = jnp.zeros((rows, rows), jnp.float32)
    begin = jnp.int32(0)
    for a in range(arcs):
        end = begin + lengths[0, a]
        inside = jnp.logical_and(position >= begin, position < end)
        phi = jnp.where(inside, decays[0, a], phi)
        amp = jnp.where(inside, amps[0, a], amp)
        first = jnp.where(jnp.logical_and(inside, position == begin), 1.0, first)
        begin = end
    phi_m[...] = jnp.where(first > 0.5, 0.0, phi)
    amp_m[...] = jnp.where(first > 0.5, amp, amp * (1.0 - phi * phi))
    start_m[...] = jnp.where(position == lane, 1.0, 0.0)

    def step(k, carry):
        state, spread = carry
        at = pl.ds(k, 1)
        rate, live, floor = phi_m[at, :], live_m[at, :], noise_m[at, :]
        state = rate * state
        spread = rate * rate * spread + amp_m[at, :]
        var = spread * live + floor
        ratio = 1.0 / var
        inno = live * (start_m[at, :] - state)
        inno_m[at, :] = inno
        var_m[at, :] = var
        return state + (spread * live * ratio) * inno, spread * floor * ratio

    zero = jnp.zeros((1, rows), jnp.float32)
    lax.fori_loop(0, rows, step, (zero, zero), unroll=8)
    inverse = inno_m[...] / jnp.sqrt(var_m[...])
    high = inverse.astype(jnp.bfloat16)
    rest = inverse - high.astype(jnp.float32)
    mid = rest.astype(jnp.bfloat16)
    parts[0] = high
    parts[1] = mid
    parts[2] = (rest - mid.astype(jnp.float32)).astype(jnp.bfloat16)

    def slot(s, _):
        column = pl.multiple_of(tile_map[s] * rows, rows)
        tile = design[:, pl.ds(column, rows)]
        solved = jnp.dot(parts[2], tile, preferred_element_type=jnp.float32)
        solved += jnp.dot(parts[1], tile, preferred_element_type=jnp.float32)
        solved += jnp.dot(parts[0], tile, preferred_element_type=jnp.float32)
        place = lax.rem(s, half_tiles)
        piece = s // half_tiles
        white[piece // 2, lax.rem(piece, 2), :, pl.ds(pl.multiple_of(place * rows, rows), rows)] = (
            solved.astype(jnp.bfloat16)
        )
        low = pl.multiple_of(lax.rem(s, row_tiles) * rows, rows)
        white_t[s // row_tiles, pl.ds(low, rows), :] = jnp.transpose(solved).astype(jnp.bfloat16)
        return 0

    lax.fori_loop(0, slots_z, slot, 0, unroll=4)
    obs_m = by_row(obs[...], rows)
    solved_obs = jnp.sum(jnp.transpose(inverse) * obs_m, axis=0, keepdims=True)
    o_high = solved_obs.astype(jnp.bfloat16).astype(jnp.float32)
    o_rest = solved_obs - o_high
    o_mid = o_rest.astype(jnp.bfloat16).astype(jnp.float32)
    which = lax.broadcasted_iota(jnp.int32, (EXTRA, rows), 0)
    packed = jnp.where(which == 0, o_high, 0.0)
    packed = jnp.where(which == 1, o_mid, packed)
    packed = jnp.where(which == 2, o_rest - o_mid, packed).astype(jnp.bfloat16)
    for r in range(white_t.shape[0]):
        white_t[r, row_tiles * rows :, :] = packed


def gram_kernel(R, C, w, wt, gram, rhs, obs, rp, cp, *sems):
    (r1s, r1r, ups, upr, dns, dnr, c1s, c1r, c2s, c2r, c3s, c3r) = sems
    r, z = lax.axis_index("row"), lax.axis_index("col")
    bits = [1 << i for i in range(1, (R - 1).bit_length())]
    orders = (bits, bits[::-1])
    M = gram.shape[0]

    def flip(mask):
        out = r
        bit = 1
        while bit <= mask:
            if mask & bit:
                out = out + bit - 2 * bit * lax.rem(r // bit, 2)
            bit *= 2
        return out

    zof = lambda d: lax.rem(z + (d % C), C)
    blk = lambda mask, d: flip(mask) * C + zof(d)
    own = r * C + z

    barrier = pltpu.get_barrier_semaphore()
    for mask in range(1, R):
        pl.semaphore_signal(barrier, inc=1, device_id=(flip(mask), z), device_id_type=MESH)
    for d in range(1, C):
        pl.semaphore_signal(barrier, inc=1, device_id=(r, zof(d)), device_id_type=MESH)
    pl.semaphore_wait(barrier, R - 1 + C - 1)

    sent = []

    def send(src, dst, ss, rs, to):
        copy = pltpu.make_async_remote_copy(
            src_ref=src, dst_ref=dst, send_sem=ss, recv_sem=rs, device_id=to, device_id_type=MESH
        )
        copy.start()
        sent.append(copy)

    def arrived(dst, ss, rs):
        pltpu.make_async_remote_copy(
            src_ref=dst, dst_ref=dst, send_sem=ss, recv_sem=rs, device_id=(r, z), device_id_type=MESH
        ).wait_recv()

    def reach(d):
        long, short = C // 2, C - 1 - C // 2
        return (long, short) if d % 2 == 0 else (short, long)

    def ring(d, hop, way):
        at = blk(d, -hop if way > 0 else hop)
        src = wt.at[r] if d == 0 and hop == 0 else rp.at[at]
        ss, rs = (ups, upr) if way > 0 else (dns, dnr)
        send(src, rp.at[at], ss.at[d, hop], rs.at[d, hop], (r, zof(way)))

    def ring_wait(d, hop, way):
        at = blk(d, -(hop + 1) if way > 0 else hop + 1)
        ss, rs = (ups, upr) if way > 0 else (dns, dnr)
        arrived(rp.at[at], ss.at[d, hop], rs.at[d, hop])

    def start_rings(d):
        up, down = reach(d)
        if up > 0:
            ring(d, 0, 1)
        if down > 0:
            ring(d, 0, -1)

    def plane(mask, dz, h, k):
        at = blk(mask, dz)
        bit = orders[h][k]
        src = w.at[z, h] if mask == 0 and dz == 0 else cp.at[at, h]
        i = (mask | bit) // 2
        send(src, cp.at[at, h], c2s.at[h, i, dz], c2r.at[h, i, dz], (flip(bit), z))

    def plane_wait(mask, dz, h):
        i = mask // 2
        arrived(cp.at[blk(mask, dz), h], c2s.at[h, i, dz], c2r.at[h, i, dz])

    def partner(mask, dz):
        at = blk(mask, dz)
        src = w.at[z] if mask == 0 and dz == 0 else cp.at[at]
        send(src, cp.at[at], c3s.at[mask // 2, dz], c3r.at[mask // 2, dz], (flip(1), z))

    def spread(dz):
        for k in range(len(bits)):
            for h in (0, 1):
                plane(0, dz, h, k)
        partner(0, dz)

    zs = sorted(range(C), key=lambda d: (min(d, C - d), d))
    masks = sorted(range(R), key=lambda m: (bin(m >> 1).count("1"), m))
    for d in zs[1:]:
        send(w.at[zof(d)], cp.at[own], c1s.at[d], c1r.at[d], (r, zof(d)))
    for mask in masks[1:]:
        send(wt.at[flip(mask)], rp.at[own], r1s.at[mask], r1r.at[mask], (flip(mask), z))
    spread(0)
    start_rings(0)
    rp[own] = wt[r]
    cp[own] = w[z]
    for i in range(max(R, C)):
        if 0 < i < R:
            mask = masks[i]
            arrived(rp.at[blk(mask, 0)], r1s.at[mask], r1r.at[mask])
            start_rings(mask)
        if 0 < i < C:
            d = zs[i]
            arrived(cp.at[blk(0, -d)], c1s.at[d], c1r.at[d])
            spread((-d) % C)

    ring_jobs = []
    for hop in range(1, C):
        for d in masks:
            up, down = reach(d)
            if hop < up:
                ring_jobs.append((d, hop, 1))
            if hop < down:
                ring_jobs.append((d, hop, -1))
    plane_jobs = []
    even = [m for m in masks if m % 2 == 0]
    for m in even[1:]:
        for dz in zs:
            plane_jobs.append((m, dz))
    done_ring = set()
    for i in range(max(len(ring_jobs), len(plane_jobs))):
        if i < len(plane_jobs):
            m, dz = plane_jobs[i]
            for h in (0, 1):
                plane_wait(m, dz, h)
                last = max(orders[h].index(b) for b in orders[h] if m & b)
                for k in range(last + 1, len(bits)):
                    plane(m, dz, h, k)
            partner(m, dz)
        if i < len(ring_jobs):
            d, hop, way = ring_jobs[i]
            ring_wait(d, hop - 1, way)
            done_ring.add((d, hop - 1, way))
            ring(d, hop, way)

    K = rp.shape[2]
    half = cp.shape[3]
    wide = 256 if half % 256 == 0 else 128
    seen_row, fresh = set(), True
    order = sorted(
        [(m, dz) for m in even for dz in range(C)],
        key=lambda t: (max(bin(t[0]).count("1"), min(t[1], C - t[1])), t[0], t[1]),
    )
    for m, dz in order:
        for d in (m, m | 1):
            if dz != 0:
                up, down = reach(d)
                item = (d, dz - 1, -1) if dz <= down else (d, C - dz - 1, 1)
                if item not in done_ring:
                    ring_wait(*item)
                    done_ring.add(item)
        arrived(cp.at[blk(m | 1, dz)], c3s.at[m // 2, dz], c3r.at[m // 2, dz])
        b0, b1 = blk(m, dz), blk(m | 1, dz)
        left = jnp.concatenate([rp[b0, :M, :], rp[b1, :M, :]], axis=1)
        seen = jnp.concatenate([rp[b0, M:, :], rp[b1, M:, :]], axis=1)
        obs[b0] = rp[b0, M:, :]
        obs[b1] = rp[b1, M:, :]
        side = lax.dot_general(
            seen, left, (((1,), (1,)), ((), ())), preferred_element_type=jnp.float32
        )
        if fresh:
            rhs[...] = side
        else:
            rhs[...] += side

        for h in (0, 1):

            def tile(j, _, h=h, b0=b0, b1=b1, fresh=fresh):
                at = pl.ds(pl.multiple_of(j * wide, wide), wide)
                to = pl.ds(pl.multiple_of(h * half + j * wide, wide), wide)
                lhs = jnp.concatenate([rp[b0, :M, :], rp[b1, :M, :]], axis=1)
                right = jnp.concatenate([cp[b0, h, :, at], cp[b1, h, :, at]], axis=0)
                part = jnp.dot(lhs, right, preferred_element_type=jnp.float32)
                if fresh:
                    gram[:, to] = part
                else:
                    gram[:, to] += part
                return 0

            lax.fori_loop(0, half // wide, tile, 0)
        fresh = False
    for copy in sent:
        copy.wait_send()


def on_device(R, C, design, observations, gaps, noise_var, lengths, amps, decays, plan, tile_map):
    rows, columns = design.shape
    tiles = tile_map.shape[0]
    width = columns // C
    tall = columns // R
    blocks = R * C
    vm = pl.BlockSpec(memory_space=pltpu.VMEM)
    sm = pl.BlockSpec(memory_space=pltpu.SMEM)
    square = pltpu.VMEM((rows, rows), jnp.float32)
    w, wt = pl.pallas_call(
        functools.partial(whiten_kernel, lengths.shape[1]),
        out_shape=(
            jax.ShapeDtypeStruct((C, 2, rows, width // 2), jnp.bfloat16),
            jax.ShapeDtypeStruct((R, tall + EXTRA, rows), jnp.bfloat16),
        ),
        in_specs=[sm, sm, sm, sm, vm, vm, vm, vm],
        out_specs=(vm, vm),
        scratch_shapes=[square] * 7 + [pltpu.VMEM((3, rows, rows), jnp.bfloat16)],
        name="whiten",
    )(
        tile_map, lengths, amps, decays, design,
        observations[None, :], gaps[None, :], noise_var[None, :],
    )
    dma = lambda *shape: pltpu.SemaphoreType.DMA(shape)
    sems = []
    for shape in ((R,), (R, C), (R, C), (C,), (2, R // 2, C), (R // 2, C)):
        sems += [dma(*shape), dma(*shape)]
    gram, rhs, obs = pl.pallas_call(
        functools.partial(gram_kernel, R, C),
        out_shape=(
            jax.ShapeDtypeStruct((tall, width), jnp.float32),
            jax.ShapeDtypeStruct((EXTRA, tall), jnp.float32),
            jax.ShapeDtypeStruct((blocks, EXTRA, rows), jnp.bfloat16),
        ),
        in_specs=[vm, vm],
        out_specs=(vm, vm, vm),
        scratch_shapes=[
            pltpu.VMEM((blocks, tall + EXTRA, rows), jnp.bfloat16),
            pltpu.VMEM((blocks, 2, rows, width // 2), jnp.bfloat16),
        ]
        + sems,
        compiler_params=pltpu.CompilerParams(
            collective_id=0, has_side_effects=True, vmem_limit_bytes=63 * 1024 * 1024
        ),
        name="gram",
    )(w, wt)
    picked = jnp.take(obs, plan, axis=0).astype(jnp.float32)
    balanced = picked[:, 0] + (picked[:, 1] + picked[:, 2])
    return gram, rhs[0], balanced


def solution(mesh):
    both = ("row", "col")
    placed = (
        P(both, None), P(both), P(both), P(both), P(both, None), P(both, None), P(both, None),
        P(both), P(),
    )
    return jax.shard_map(
        functools.partial(on_device, mesh.shape["row"], mesh.shape["col"]),
        mesh=mesh,
        in_specs=placed,
        out_specs=(P("row", "col"), P("row"), P(both, None)),
        check_vma=False,
    )
```

time: 325 us -> 172 us (0.53)
  blocking collectives: 175 us -> 0 us
  Pallas kernels: 0 us -> 163 us
  local copies, waits for them, and re-layouts: 46.9 us -> 6.18 us
  waiting for transfers between devices: 31.6 us -> 0 us
  other arithmetic: 28.8 us -> 1.2 us
  matrix products: 25.6 us -> 0 us
  between operations: 14.8 us -> 1.3 us
    pallas_call x0 -> x2, Pallas kernels: none -> 163 us  [the longest x1 154 us: on_device(): pl.pallas_call(functools.partial(gram_kernel, R, C), out_shape=(jax.Shape...]
    all_to_all x2 -> x0, blocking collectives: 105 us -> none  [the longest x1 80.1 us: on_device(): lax.all_to_all(slotted, 'col', split_axis=1, concat_axis=0, tiled=True)]
    all_gather x1 -> x0, blocking collectives: 70 us -> none  [on_device(): lax.all_gather(white_obs.reshape(local_rows), ('row', 'col'), axis=0, til...]
    all_gather x2 -> x0, waiting for transfers between devices: 31.5 us -> none  [the longest x1 31.5 us: on_device(): shard_piece = lax.all_gather(own_cols, 'row', axis=0, tiled=True)]
    all_gather x2 -> x0, local copies, waits for them, and re-layouts: 25.8 us -> none  [the longest x1 16.8 us: on_device(): shard_piece = lax.all_gather(own_cols, 'row', axis=0, tiled=True)]
    another operation x6 -> x0, other arithmetic: 23.7 us -> none  [the longest x3 12.4 us: whiten(): factor = jnp.linalg.cholesky(covariance)]
    dot_general x2 -> x0, matrix products: 21.1 us -> none  [the longest x1 16.2 us: on_device(): lax.dot_general(row_panel, flat_piece, (((0,), (0,)), ((), ())), preferre...]
    transpose x1 -> x0, local copies, waits for them, and re-layouts: 9.09 us -> none  [on_device(): jnp.swapaxes(row_panel, 0, 1).reshape(total_rows, row_tiles * tile_size)]
  transfers between devices with their start and end apart: 2 -> 0, of which waited for: 1 -> 0; matrix products, arithmetic and copies ran while one was open for 10% -> 0% of each run, Pallas kernels for 0% -> 0%
where the time goes in v1:
time: 172 us; the launch traced here: 171 us
  Pallas kernels  163 us (95%)
  local copies, waits for them, and re-layouts  6.18 us (4%)
    pallas_call x1, Pallas kernels, on_device(): pl.pallas_call(functools.partial(gram_kernel, R, C), out_shape=(jax.Shape...  154 us
    pallas_call x1, Pallas kernels, on_device(): pl.pallas_call(functools.partial(whiten_kernel, lengths.shape[1]), out_sh...  8.92 us
    unnamed x1, local copies, waits for them, and re-layouts  4.84 us

profile of v1, /device:TPU:8, one launch (start us, length us, event | category | flops | bytes accessed | tf_op | source)
XLA Modules:
  0.0 171.5 jit_solution(6420054286148898934)
XLA Ops:
  1.3 8.9 %whiten.1 = (bf16[4,2,128,768]{3,2,1,0:T(8,128)(2,1)}, bf16[8,784,128]{2,1,0:T(8,128)(2,1)}) custom-call(s32[48]{0:T(128)} %tile_map.1, s32[1,4]{1,0:T(1,128)} %lengths.1, f32[1,4]{1,0:T(1,128)} %amps.1, f32[1,4]{1,0:T(1,128)} %decays.1, bf16[128,6144]{1,0:T(8,128)(2,1)} %design.1, f32[1,128]{1,0:T(1,128)} %bitcast.7, s32[1,128]{1,0:T(1,128)} %bitcast.8, ...), custom_call_target="tpu_custom_call" | custom-call | tf_op jit(solution)/shard_map/whiten/pallas_call | solution.py:291
  10.2 153.9 %gram.1 = (f32[768,1536]{1,0:T(8,128)}, f32[16,768]{1,0:T(8,128)}, bf16[32,16,128]{2,1,0:T(8,128)(2,1)}) custom-call(bf16[4,2,128,768]{3,2,1,0:T(8,128)(2,1)} %get-tuple-element.8.w, bf16[8,784,128]{2,1,0:T(8,128)(2,1)} %get-tuple-element.9.wt), custom_call_target="tpu_custom_call" | custom-call | tf_op jit(solution)/shard_map/gram/pallas_call | solution.py:309
  164.1 0.7 fusion
  164.8 0.5 fusion.2
  165.3 1.3 slice_reduce_fusion
  166.6 4.8 %copy.14 = f32[768,1536]{1,0:T(8,128)} copy(f32[768,1536]{1,0:T(8,128)} %get-tuple-element.27) | data formatting | bytes 9437184

commit v2 on v1

v2 whole, which is shorter than its diff:
```python
import functools

import jax
import jax.numpy as jnp
from jax import lax
from jax.experimental import pallas as pl
from jax.experimental.pallas import tpu as pltpu
from jax.sharding import PartitionSpec as P

MESH = pl.DeviceIdType.MESH
EXTRA = 16


def by_row(vector, rows):
    return jnp.transpose(jnp.broadcast_to(vector, (rows, vector.shape[1])))


def whiten_kernel(
    arcs, tile_map, lengths, amps, decays, design, obs, gaps, noise,
    white_t, live_m, noise_m, phi_m, amp_m, start_m, inno_m, var_m, parts,
):
    rows = design.shape[0]
    slots = design.shape[1] // rows
    row_tiles = (white_t.shape[1] - EXTRA) // rows
    live_row = gaps[...].astype(jnp.float32)
    live_m[...] = by_row(live_row, rows)
    noise_m[...] = by_row(noise[...], rows)
    position = lax.broadcasted_iota(jnp.int32, (rows, rows), 0)
    lane = lax.broadcasted_iota(jnp.int32, (rows, rows), 1)
    phi = jnp.zeros((rows, rows), jnp.float32)
    amp = jnp.zeros((rows, rows), jnp.float32)
    first = jnp.zeros((rows, rows), jnp.float32)
    begin = jnp.int32(0)
    for a in range(arcs):
        end = begin + lengths[0, a]
        inside = jnp.logical_and(position >= begin, position < end)
        phi = jnp.where(inside, decays[0, a], phi)
        amp = jnp.where(inside, amps[0, a], amp)
        first = jnp.where(jnp.logical_and(inside, position == begin), 1.0, first)
        begin = end
    phi_m[...] = jnp.where(first > 0.5, 0.0, phi)
    amp_m[...] = jnp.where(first > 0.5, amp, amp * (1.0 - phi * phi))
    start_m[...] = jnp.where(position == lane, 1.0, 0.0)

    def step(k, carry):
        state, spread = carry
        at = pl.ds(k, 1)
        rate, live, floor = phi_m[at, :], live_m[at, :], noise_m[at, :]
        state = rate * state
        spread = rate * rate * spread + amp_m[at, :]
        var = spread * live + floor
        ratio = 1.0 / var
        inno = live * (start_m[at, :] - state)
        inno_m[at, :] = inno
        var_m[at, :] = var
        return state + (spread * live * ratio) * inno, spread * floor * ratio

    zero = jnp.zeros((1, rows), jnp.float32)
    lax.fori_loop(0, rows, step, (zero, zero), unroll=8)
    inverse = inno_m[...] / jnp.sqrt(var_m[...])
    high = inverse.astype(jnp.bfloat16)
    rest = inverse - high.astype(jnp.float32)
    mid = rest.astype(jnp.bfloat16)
    parts[0] = high
    parts[1] = mid
    parts[2] = (rest - mid.astype(jnp.float32)).astype(jnp.bfloat16)

    def slot(s, _):
        column = pl.multiple_of(tile_map[s] * rows, rows)
        tile = design[:, pl.ds(column, rows)]
        solved = jnp.dot(parts[2], tile, preferred_element_type=jnp.float32)
        solved += jnp.dot(parts[1], tile, preferred_element_type=jnp.float32)
        solved += jnp.dot(parts[0], tile, preferred_element_type=jnp.float32)
        low = pl.multiple_of(lax.rem(s, row_tiles) * rows, rows)
        white_t[s // row_tiles, pl.ds(low, rows), :] = jnp.transpose(solved).astype(jnp.bfloat16)
        return 0

    lax.fori_loop(0, slots, slot, 0, unroll=4)
    obs_m = by_row(obs[...], rows)
    solved_obs = jnp.sum(jnp.transpose(inverse) * obs_m, axis=0, keepdims=True)
    o_high = solved_obs.astype(jnp.bfloat16).astype(jnp.float32)
    o_rest = solved_obs - o_high
    o_mid = o_rest.astype(jnp.bfloat16).astype(jnp.float32)
    which = lax.broadcasted_iota(jnp.int32, (EXTRA, rows), 0)
    packed = jnp.where(which == 0, o_high, 0.0)
    packed = jnp.where(which == 1, o_mid, packed)
    packed = jnp.where(which == 2, o_rest - o_mid, packed).astype(jnp.bfloat16)
    for r in range(white_t.shape[0]):
        white_t[r, row_tiles * rows :, :] = packed


def xor(a, b, limit):
    out, bit = 0, 1
    while bit < limit:
        out = out + bit * lax.rem(a // bit + b // bit, 2)
        bit *= 2
    return out


def gram_kernel(R, C, wt, gram, rhs, obs, rp, cp, *sems):
    (r1s, r1r, ups, upr, dns, dnr, chs, chr_, pas, par) = sems
    r, z = lax.axis_index("row"), lax.axis_index("col")
    M = gram.shape[0]
    G = R // 2
    core, chip = lax.rem(r, 2), r // 2

    def flip(mask):
        return xor(r, mask, R)

    zof = lambda d: lax.rem(z + (d % C), C)
    blk = lambda mask, d: flip(mask) * C + zof(d)
    apart = xor(chip, z, G)
    place, shift = apart, 2
    while shift <= G:
        place = xor(place, apart // shift, G)
        shift *= 2

    def seat(p):
        return 2 * xor(xor(p, p // 2, G), z, G) + core

    ahead = (seat(lax.rem(place + 1, G)), seat(lax.rem(place + G - 1, G)))
    steps = (place, lax.rem(G - place, G))

    barrier = pltpu.get_barrier_semaphore()
    for mask in range(1, R):
        pl.semaphore_signal(barrier, inc=1, device_id=(flip(mask), z), device_id_type=MESH)
    for d in range(1, C):
        pl.semaphore_signal(barrier, inc=1, device_id=(r, zof(d)), device_id_type=MESH)
    pl.semaphore_wait(barrier, R - 1 + C - 1)

    sent = []

    def remote(src, dst, ss, rs, to):
        return pltpu.make_async_remote_copy(
            src_ref=src, dst_ref=dst, send_sem=ss, recv_sem=rs, device_id=to, device_id_type=MESH
        )

    def send(*args):
        copy = remote(*args)
        copy.start()
        sent.append(copy)

    def arrived(dst, ss, rs):
        remote(dst, dst, ss, rs, (r, z)).wait_recv()

    def reach(d):
        long, short = C // 2, C - 1 - C // 2
        return (long, short) if d % 2 == 0 else (short, long)

    def ring(d, hop, way):
        at = blk(d, -hop if way > 0 else hop)
        src = wt.at[r] if d == 0 and hop == 0 else rp.at[at]
        ss, rs = (ups, upr) if way > 0 else (dns, dnr)
        send(src, rp.at[at], ss.at[d, hop], rs.at[d, hop], (r, zof(way)))

    def block_of(h, mask, dz):
        return xor(2 * z + h, mask, R) * C + zof(dz)

    def chain(src, mask, dz):
        at = block_of(core, mask, dz)
        return remote(
            src, cp.at[core, at], chs.at[mask, dz], chr_.at[mask, dz], (ahead[mask % 2], z)
        )

    def partner(src, mask, dz):
        at = block_of(core, mask, dz)
        return remote(src, cp.at[core, at], pas.at[mask, dz], par.at[mask, dz], (flip(1), z))

    def take(mask, dz):
        at = blk(mask, dz)
        if dz == 0:
            if mask:
                arrived(rp.at[at], r1s.at[mask], r1r.at[mask])
            up, down = reach(mask)
            if up > 0:
                ring(mask, 0, 1)
            if down > 0:
                ring(mask, 0, -1)
        else:
            up, down = reach(mask)
            if dz <= down:
                hop, way, last, ss, rs = dz - 1, -1, down, dns, dnr
            else:
                hop, way, last, ss, rs = C - dz - 1, 1, up, ups, upr
            arrived(rp.at[at], ss.at[mask, hop], rs.at[mask, hop])
            if hop + 1 < last:
                ring(mask, hop + 1, way)

        @pl.when(place == 0)
        def _():
            src = wt.at[r, :M] if mask == 0 and dz == 0 else rp.at[at, :M]
            chain(src, mask, dz).start()
            partner(src, mask, dz).start()
            cp[core, at] = rp[at, :M, :]

    def relay(mask, dz):
        at = block_of(core, mask, dz)

        @pl.when(place > 0)
        def _():
            src = cp.at[core, at]
            arrived(src, chs.at[mask, dz], chr_.at[mask, dz])

            @pl.when(steps[mask % 2] < G - 1)
            def _():
                chain(src, mask, dz).start()

            partner(src, mask, dz).start()

    K = rp.shape[2]
    wide = 256 if M % 256 == 0 else 128

    def accumulate(q, dz, fresh):
        b0 = 2 * q * C + zof(dz)
        b1 = b0 + C
        left = jnp.concatenate([rp[b0, :M, :], rp[b1, :M, :]], axis=1)
        seen = jnp.concatenate([rp[b0, M:, :], rp[b1, M:, :]], axis=1)
        obs[b0] = rp[b0, M:, :]
        obs[b1] = rp[b1, M:, :]
        nt = (((1,), (1,)), ((), ()))
        side = lax.dot_general(seen, left, nt, preferred_element_type=jnp.float32)
        if fresh:
            rhs[...] = side
        else:
            rhs[...] += side
        for h in (0, 1):

            def tile(j, _, h=h):
                at = pl.ds(pl.multiple_of(j * wide, wide), wide)
                to = pl.ds(pl.multiple_of(h * M + j * wide, wide), wide)
                lhs = jnp.concatenate([rp[b0, :M, :], rp[b1, :M, :]], axis=1)
                right = jnp.concatenate([cp[h, b0, at, :], cp[h, b1, at, :]], axis=1)
                part = lax.dot_general(lhs, right, nt, preferred_element_type=jnp.float32)
                if fresh:
                    gram[:, to] = part
                else:
                    gram[:, to] += part
                return 0

            lax.fori_loop(0, M // wide, tile, 0)

    masks = sorted(range(R), key=lambda m: (bin(m >> 1).count("1"), m))
    zs = sorted(range(C), key=lambda d: (min(d, C - d), d))
    for mask in masks[1:]:
        send(wt.at[flip(mask)], rp.at[r * C + z], r1s.at[mask], r1r.at[mask], (flip(mask), z))
    rp[r * C + z] = wt[r]
    items = [(mask, dz) for dz in zs for mask in masks]
    lag = 3
    for i in range(len(items) + lag):
        if i < len(items):
            take(*items[i])
        if i >= lag:
            j = i - lag
            relay(*items[j])
            phase, inside = divmod(j, R)
            if phase > 0 and inside % 2 == 1:
                if inside == 1:
                    for mask in masks:
                        dz = zs[phase - 1]
                        at = block_of(1 - core, mask, dz)
                        arrived(cp.at[1 - core, at], pas.at[mask, dz], par.at[mask, dz])
                accumulate(inside // 2, zs[phase - 1], phase == 1 and inside == 1)
    dz = zs[-1]
    for mask in masks:
        at = block_of(1 - core, mask, dz)
        arrived(cp.at[1 - core, at], pas.at[mask, dz], par.at[mask, dz])
    for q in range(G):
        accumulate(q, dz, False)
    for mask, dz in items:
        src = cp.at[core, block_of(core, mask, dz)]
        partner(src, mask, dz).wait_send()

        @pl.when(steps[mask % 2] < G - 1)
        def _():
            chain(src, mask, dz).wait_send()

    for copy in sent:
        copy.wait_send()


def on_device(R, C, design, observations, gaps, noise_var, lengths, amps, decays, plan, tile_map):
    rows, columns = design.shape
    tiles = tile_map.shape[0]
    width = columns // C
    tall = columns // R
    blocks = R * C
    vm = pl.BlockSpec(memory_space=pltpu.VMEM)
    sm = pl.BlockSpec(memory_space=pltpu.SMEM)
    square = pltpu.VMEM((rows, rows), jnp.float32)
    wt = pl.pallas_call(
        functools.partial(whiten_kernel, lengths.shape[1]),
        out_shape=jax.ShapeDtypeStruct((R, tall + EXTRA, rows), jnp.bfloat16),
        in_specs=[sm, sm, sm, sm, vm, vm, vm, vm],
        out_specs=vm,
        scratch_shapes=[square] * 7 + [pltpu.VMEM((3, rows, rows), jnp.bfloat16)],
        name="whiten",
    )(
        tile_map, lengths, amps, decays, design,
        observations[None, :], gaps[None, :], noise_var[None, :],
    )
    dma = lambda *shape: pltpu.SemaphoreType.DMA(shape)
    sems = []
    for shape in ((R,), (R, C), (R, C), (R, C), (R, C)):
        sems += [dma(*shape), dma(*shape)]
    gram, rhs, obs = pl.pallas_call(
        functools.partial(gram_kernel, R, C),
        out_shape=(
            jax.ShapeDtypeStruct((tall, width), jnp.float32),
            jax.ShapeDtypeStruct((EXTRA, tall), jnp.float32),
            jax.ShapeDtypeStruct((blocks, EXTRA, rows), jnp.bfloat16),
        ),
        in_specs=[vm],
        out_specs=(vm, vm, vm),
        scratch_shapes=[
            pltpu.VMEM((blocks, tall + EXTRA, rows), jnp.bfloat16),
            pltpu.VMEM((2, blocks, tall, rows), jnp.bfloat16),
        ]
        + sems,
        compiler_params=pltpu.CompilerParams(
            collective_id=0, has_side_effects=True, vmem_limit_bytes=63 * 1024 * 1024
        ),
        name="gram",
    )(wt)
    picked = jnp.take(obs, plan, axis=0).astype(jnp.float32)
    balanced = picked[:, 0] + (picked[:, 1] + picked[:, 2])
    return gram, rhs[0], balanced


def solution(mesh):
    both = ("row", "col")
    placed = (
        P(both, None), P(both), P(both), P(both), P(both, None), P(both, None), P(both, None),
        P(both), P(),
    )
    return jax.shard_map(
        functools.partial(on_device, mesh.shape["row"], mesh.shape["col"]),
        mesh=mesh,
        in_specs=placed,
        out_specs=(P("row", "col"), P("row"), P(both, None)),
        check_vma=False,
    )
```

time: 172 us -> 400 us (2.33)
  Pallas kernels: 163 us -> 390 us
    pallas_call x1, Pallas kernels: 154 us -> 382 us  [on_device(): pl.pallas_call(functools.partial(gram_kernel, R, C), out_shape=(jax.Shape...]
where the time goes in v2:
time: 400 us; the launch traced here: 399 us
  Pallas kernels  390 us (98%)
  local copies, waits for them, and re-layouts  6.18 us (2%)
    pallas_call x1, Pallas kernels, on_device(): pl.pallas_call(functools.partial(gram_kernel, R, C), out_shape=(jax.Shape...  382 us
    pallas_call x1, Pallas kernels, on_device(): pl.pallas_call(functools.partial(whiten_kernel, lengths.shape[1]), out_sh...  8.59 us

profile of v2, /device:TPU:8, one launch (start us, length us, event | category | flops | bytes accessed | tf_op | source)
XLA Modules:
  0.0 399.2 jit_solution(10030290657367205565)
XLA Ops:
  1.3 8.6 %whiten.1.wt = bf16[8,784,128]{2,1,0:T(8,128)(2,1)} custom-call(s32[48]{0:T(128)} %tile_map.1, s32[1,4]{1,0:T(1,128)} %lengths.1, f32[1,4]{1,0:T(1,128)} %amps.1, f32[1,4]{1,0:T(1,128)} %decays.1, bf16[128,6144]{1,0:T(8,128)(2,1)} %design.1, f32[1,128]{1,0:T(1,128)} %bitcast.7, s32[1,128]{1,0:T(1,128)} %bitcast.8, f32[1,128]{1,0:T(1,128)} %bitcast.9), custom_call_target="tpu_custom_call" | custom-call | tf_op jit(solution)/shard_map/whiten/pallas_call | solution.py:290
  9.9 381.9 %gram.1 = (f32[768,1536]{1,0:T(8,128)}, f32[16,768]{1,0:T(8,128)}, bf16[32,16,128]{2,1,0:T(8,128)(2,1)}) custom-call(bf16[8,784,128]{2,1,0:T(8,128)(2,1)} %whiten.1.wt), custom_call_target="tpu_custom_call" | custom-call | tf_op jit(solution)/shard_map/gram/pallas_call | solution.py:305
  391.8 0.7 fusion
  392.5 0.5 fusion.2
  393.0 1.3 slice_reduce_fusion
  394.3 4.8 %copy.14 = f32[768,1536]{1,0:T(8,128)} copy(f32[768,1536]{1,0:T(8,128)} %get-tuple-element.23) | data formatting | bytes 9437184
